TPU v7x, 256 devices: a whole 4x4x8 slice. The times are simulated.
256 devices in a mesh: dp: 64 (over z, x, core), layer: 4 (over y).
Axes of the slice: x: 4, y: 4, z: 8, core: 2. Of those that a mesh axis runs over, the one named last changes fastest.
Arguments:
- acts: bfloat16 [4, 57344, 4608], P('layer', 'dp')
- probes: bfloat16 [4, 4608, 512], P('layer'), may hold values from -0.25 to 0.25
- labels: int32 [57344], P('dp'), may hold values from 0 to 511
Outputs:
- grads: float32 [4, 4608, 512], P('layer', 'dp')
- losses: float32 [4], P('layer')
All inputs are finite; a program needn't handle non-finite values.
Results may differ from a plain program's by a relative error of at most 0.0013.
Values sent between devices are 32-bit elements; how exact they have to be, the bound alone decides.
A program may use at most 128 MiB of HBM per device.

v0:
```python
import jax
import jax.numpy as jnp
from jax import lax
from jax.sharding import Mesh
from jax.sharding import PartitionSpec as P

DP = ("dp_0", "dp_1", "dp_2")


def cut_along(x, dim, length):
    shape = x.shape
    pieces = x.reshape(*shape[:dim], length, shape[dim] // length, *shape[dim + 1 :])
    return jnp.moveaxis(pieces, dim, 0)


def summed_on_arrival(x, axis, dim):
    pieces = cut_along(x, dim, lax.axis_size(axis))
    arrived = lax.all_to_all(pieces, axis, split_axis=0, concat_axis=0, tiled=True)
    return arrived.sum(axis=0)


def sum_in_two_steps(x, axes, dim):
    far, near = axes
    pieces = cut_along(x, dim, lax.axis_size(far))
    nearer = summed_on_arrival(pieces, near, dim + 1)
    arrived = lax.all_to_all(nearer, far, split_axis=0, concat_axis=0, tiled=True)
    return arrived.sum(axis=0)


def copy_for_each(x, axis):
    copies = jnp.broadcast_to(x, (lax.axis_size(axis), *x.shape))
    return lax.all_to_all(copies, axis, split_axis=0, concat_axis=0, tiled=True)


def of_everyone(x, axis):
    everything = copy_for_each(x, axis)
    return jnp.sum(everything, axis=0)


def layer_terms(acts_l, probe_l, onehot):
    logits = jnp.dot(acts_l, probe_l, preferred_element_type=jnp.float32)
    top = jnp.max(logits, axis=1, keepdims=True)
    expo = jnp.exp(logits - top)
    total = jnp.sum(expo, axis=1, keepdims=True)
    probs = expo / total
    lse = top[:, 0] + jnp.log(total[:, 0])
    picked = jnp.sum(onehot * logits, axis=1)
    resid = (probs - onehot).astype(jnp.bfloat16)
    return (resid, jnp.sum(lse - picked))


def per_device(acts, probes, labels):
    shards = lax.axis_size(DP)
    tok_rows = acts.shape[1]
    count_all = tok_rows * shards
    factor = jnp.float32(1.0 / count_all**0.5)
    classes = jnp.arange(probes.shape[2], dtype=jnp.int32)
    onehot = (labels[:, None] == classes[None, :]).astype(jnp.float32)
    resid, loss_part = layer_terms(acts[0], probes[0], onehot)
    partial_value = [loss_part]
    terms = jnp.stack(
        [
            lax.dot_general(
                acts[0], resid, (((0,), (0,)), ((), ())), preferred_element_type=jnp.float32
            )
            * factor
        ]
    )
    grads = sum_in_two_steps(terms, (("dp_0", "dp_1"), "dp_2"), 1)
    summed = of_everyone(jnp.stack(partial_value), DP)
    losses = summed / jnp.float32(count_all)
    return (grads, losses)


def solution(mesh):
    torus = Mesh(
        mesh.devices.reshape(8, 4, 2, mesh.shape["layer"]), ("dp_0", "dp_1", "dp_2", "layer")
    )
    in_specs = (P("layer", DP, None), P("layer", None, None), P(DP))
    out_specs = (P("layer", DP, None), P("layer"))
    return jax.shard_map(
        per_device, mesh=torus, in_specs=in_specs, out_specs=out_specs, check_vma=False
    )
```

profile of v0, /device:TPU:27, one launch (start us, length us, event | category | flops | bytes accessed | tf_op | source)
XLA Modules:
  0.0 197.2 jit_solution(11337564156793117061)
XLA Ops:
  0.6 0.0 copy-start
  0.6 0.0 copy-start.1
  0.7 9.7 %fusion.8 = (f32[896]{0:T(1024)S(1)}, f32[896,512]{0,1:T(8,128)S(1)}) fusion(bf16[1,4608,512]{2,1,0:T(8,128)(2,1)} %param.4, bf16[1,896,4608]{2,1,0:T(8,128)(2,1)} %param.3), kind=kOutput, calls=%fused_computation.14 | convolution fusion | flops 4228316160 | bytes 14814720 | tf_op jit(solution)/shard_map/dot_general | solution.py:41
  10.4 0.0 copy-done
  10.4 0.5 select_reduce_fusion
  10.9 0.0 copy-done.1
  10.9 7.9 %multiply_bitcast_fusion = f32[4608,512]{0,1:T(8,128)} fusion(bf16[1,896,4608]{2,1,0:T(8,128)(2,1)S(1)} %copy-done.1, f32[896,512]{0,1:T(8,128)S(1)} %get-tuple-element.5, s32[896]{0:T(1024)S(1)} %copy-done, f32[896]{0:T(1024)S(1)} %get-tuple-element.3, f32[896]{0:T(1024)S(1)} %get-tuple-element.4), kind=kOutput, calls=%fused_computation | convolution fusion | flops 4232970240 | bytes 19540480 | tf_op jit(solution)/shard_map/dot_general | solution.py:63
  18.8 9.6 %copy.10 = f32[4608,512]{1,0:T(8,128)} copy(f32[4608,512]{0,1:T(8,128)} %multiply_bitcast_fusion) | data formatting | bytes 18874368 | tf_op jit(solution)/shard_map/mul | solution.py:63
  28.4 8.7 %copy.11 = f32[2,32,1,72,512]{4,3,1,2,0:T(8,128)} copy(f32[2,32,1,72,512]{4,3,0,1,2:T(8,128)} %bitcast.20) | data formatting | bytes 18874368 | tf_op jit(solution)/shard_map/transpose | solution.py:13
  37.1 8.0 %all-to-all-start = ((f32[2,32,1,72,512]{4,3,1,2,0:T(8,128)}), f32[2,32,1,72,512]{4,3,1,2,0:T(8,128)}, u32[]{:S(2)}, u32[]{:S(2)}) async-start(f32[2,32,1,72,512]{4,3,1,2,0:T(8,128)} %copy.11), calls=%async_computation | async-start | bytes 18874368 | tf_op jit(solution)/shard_map/all_to_all | solution.py:18
  45.1 0.6 subtract_reduce_fusion
  45.7 7.3 %all-to-all-done = f32[2,32,1,72,512]{4,3,1,2,0:T(8,128)} async-done(((f32[2,32,1,72,512]{4,3,1,2,0:T(8,128)}), f32[2,32,1,72,512]{4,3,1,2,0:T(8,128)}, u32[]{:S(2)}, u32[]{:S(2)}) %all-to-all-start) | async-done | bytes 9437216 | tf_op jit(solution)/shard_map/all_to_all | solution.py:18
  53.0 1.3 broadcast_in_dim.2
  54.3 12.0 %all-to-all-start.2 = ((f32[64,1,1]{2,1,0:T(1,128)}), f32[64,1,1]{2,1,0:T(1,128)S(1)}, u32[]{:S(2)}, u32[]{:S(2)}) async-start(f32[64,1,1]{2,1,0:T(1,128)} %broadcast_in_dim.2), calls=%async_computation.2 | async-start | bytes 65536 | tf_op jit(solution)/shard_map/all_to_all | solution.py:32
  66.3 7.5 %reduce_sum.59 = f32[32,72,512]{2,1,0:T(8,128)} reduce(f32[2,32,1,72,512]{4,3,1,2,0:T(8,128)} %all-to-all-done, f32[]{:T(128)} %constant.8.clone.1), dimensions={0,2}, to_apply=%region_2.0 | reduce | flops 1179648 | bytes 14155780 | tf_op jit(solution)/shard_map/reduce_sum | solution.py:19
  73.8 0.8 all-to-all-done.2
  74.6 8.6 %all-to-all-start.1 = ((f32[32,1,72,512]{3,2,1,0:T(8,128)}), f32[32,1,72,512]{3,2,1,0:T(8,128)}, u32[]{:S(2)}, u32[]{:S(2)}) async-start(f32[32,1,72,512]{3,2,1,0:T(8,128)} %bitcast.21), calls=%async_computation.1 | async-start | bytes 9437184 | tf_op jit(solution)/shard_map/all_to_all | solution.py:26
  83.2 0.7 reduce_sum.65
  84.5 108.2 %all-to-all-done.1 = f32[32,1,72,512]{3,2,1,0:T(8,128)} async-done(((f32[32,1,72,512]{3,2,1,0:T(8,128)}), f32[32,1,72,512]{3,2,1,0:T(8,128)}, u32[]{:S(2)}, u32[]{:S(2)}) %all-to-all-start.1) | async-done | bytes 4718624 | tf_op jit(solution)/shard_map/all_to_all | solution.py:26
  192.7 3.4 %reduce_sum.61 = f32[72,512]{1,0:T(8,128)} reduce(f32[32,1,72,512]{3,2,1,0:T(8,128)} %all-to-all-done.1, f32[]{:T(128)} %constant.8.clone.1), dimensions={0,1}, to_apply=%region_3.0 | reduce | flops 1142784 | bytes 4866052 | tf_op jit(solution)/shard_map/reduce_sum | solution.py:27
Async XLA Ops:
  0.6 9.7 %copy-start = (s32[896]{0:T(1024)S(1)}, s32[896]{0:T(1024)}, u32[]{:S(2)}) copy-start(s32[896]{0:T(1024)} %param.5) | copy-start | bytes 10756
  0.6 10.2 %copy-start.1 = (bf16[1,896,4608]{2,1,0:T(8,128)(2,1)S(1)}, bf16[1,896,4608]{2,1,0:T(8,128)(2,1)}, u32[]{:S(2)}) copy-start(bf16[1,896,4608]{2,1,0:T(8,128)(2,1)} %param.3) | copy-start | bytes 24772612
  37.1 15.8 %all-to-all-start = ((f32[2,32,1,72,512]{4,3,1,2,0:T(8,128)}), f32[2,32,1,72,512]{4,3,1,2,0:T(8,128)}, u32[]{:S(2)}, u32[]{:S(2)}) async-start(f32[2,32,1,72,512]{4,3,1,2,0:T(8,128)} %copy.11), calls=%async_computation | async-start | bytes 18874368 | tf_op jit(solution)/shard_map/all_to_all | solution.py:18
  54.3 20.3 %all-to-all-start.2 = ((f32[64,1,1]{2,1,0:T(1,128)}), f32[64,1,1]{2,1,0:T(1,128)S(1)}, u32[]{:S(2)}, u32[]{:S(2)}) async-start(f32[64,1,1]{2,1,0:T(1,128)} %broadcast_in_dim.2), calls=%async_computation.2 | async-start | bytes 65536 | tf_op jit(solution)/shard_map/all_to_all | solution.py:32
  74.6 118.1 %all-to-all-start.1 = ((f32[32,1,72,512]{3,2,1,0:T(8,128)}), f32[32,1,72,512]{3,2,1,0:T(8,128)}, u32[]{:S(2)}, u32[]{:S(2)}) async-start(f32[32,1,72,512]{3,2,1,0:T(8,128)} %bitcast.21), calls=%async_computation.1 | async-start | bytes 9437184 | tf_op jit(solution)/shard_map/all_to_all | solution.py:26
where the time goes:
time: 198 us; the launch traced here: 197 us
  waiting for transfers between devices  116 us (59%)
  starting transfers between devices  28.6 us (14%)
  local copies, waits for them, and re-layouts  19.6 us (10%)
  matrix products  17.6 us (9%)
  other arithmetic  12.7 us (6%)
  between operations  2.48 us (1%)
    all_to_all x1, waiting for transfers between devices, sum_in_two_steps(): lax.all_to_all(nearer, far, split_axis=0, concat_axis=0, tiled=True)  108 us
    all_to_all x1, starting transfers between devices, copy_for_each(): return lax.all_to_all(copies, axis, split_axis=0, concat_axis=0, tiled=True)  12 us
    dot_general x1, matrix products, layer_terms(): logits = jnp.dot(acts_l, probe_l, preferred_element_type=jnp.float32)  9.7 us
    mul x1, local copies, waits for them, and re-layouts, per_device(): lax.dot_general(acts[0], resid, (((0,), (0,)), ((), ())), preferred_eleme...  9.63 us
    transpose x1, local copies, waits for them, and re-layouts, cut_along(): return jnp.moveaxis(pieces, dim, 0)  8.74 us
    all_to_all x1, starting transfers between devices, sum_in_two_steps(): lax.all_to_all(nearer, far, split_axis=0, concat_axis=0, tiled=True)  8.63 us
    all_to_all x1, starting transfers between devices, summed_on_arrival(): lax.all_to_all(pieces, axis, split_axis=0, concat_axis=0, tiled=True)  7.96 us
    dot_general x1, matrix products, per_device(): lax.dot_general(acts[0], resid, (((0,), (0,)), ((), ())), preferred_eleme...  7.91 us
  transfers between devices with their start and end apart: 3, of which 3 were waited for; matrix products, arithmetic and copies ran while one was open for 4% of the time, Pallas kernels for 0%

commit v1 on v0

v1 whole, which is shorter than its diff:
```python
import jax
import jax.numpy as jnp
from jax import lax
from jax.experimental import pallas as pl
from jax.experimental.pallas import tpu as pltpu
from jax.sharding import PartitionSpec as P

F32 = jnp.float32
BF16 = jnp.bfloat16
MESH = pl.DeviceIdType.MESH

NX, NZ, NC = 4, 8, 2
SHARDS = NX * NZ * NC
ROWS = 8
TILE = 16
KSTEP = 512

WIDTHS = (256, 256, 384, 256, 256, 384, 256, 256, 384)
BEHIND = {2: 1, 3: 2, 4: 3, 5: 4, 6: 5, 7: 6}


def kernel(
    tokens, depth, classes, count_all,
    acts, probes, labels,
    grads, loss,
    a, w, at, acc, resid, lab,
    snd, own, r2, xa1, xa2, za1, za, zb1, zb, xb1, xb2,
    l1, l2, l3,
    load_sem, pair_send, pair_recv, send_sem, recv_sem, loss_send, loss_recv,
):
    dp = lax.axis_index("dp")
    core = lax.rem(dp, NC)
    chip = lax.div(dp, NC)
    x = lax.rem(chip, NX)
    z = lax.div(chip, NX)
    mate = 1 - core

    def at_x(step):
        return lax.rem(x + step + NX, NX)

    def at_z(step):
        return lax.rem(z + step + NZ, NZ)

    def device(zz, xx, cc):
        return {"dp": (zz * NX + xx) * NC + cc}

    pair = device(z, x, mate)
    along_x = [device(z, at_x(step), core) for step in range(1, NX)]
    along_z = [device(at_z(step), x, core) for step in range(1, NZ)]

    barrier = pltpu.get_barrier_semaphore()
    for peer in [pair] + along_x + along_z:
        pl.semaphore_signal(barrier, inc=1, device_id=peer, device_id_type=MESH)

    steps = depth // KSTEP
    tiles = KSTEP // TILE

    def loads(k):
        columns = pl.ds(k * KSTEP, KSTEP)
        return (
            pltpu.make_async_copy(probes.at[0, columns, :], w.at[k], load_sem.at[0, k]),
            pltpu.make_async_copy(acts.at[0, :, columns], a.at[k], load_sem.at[1, k]),
        )

    for k in range(steps):
        for load in loads(k):
            load.start()

    for block in range(tokens // 128):
        row = jnp.broadcast_to(labels[block : block + 1, :], (128, 128))
        lab[block * 128 : (block + 1) * 128, :] = row.T
    acc[...] = jnp.zeros_like(acc)

    @pl.loop(0, steps)
    def _(k):
        for load in (
            pltpu.make_async_copy(probes.at[0, pl.ds(0, KSTEP), :], w.at[k], load_sem.at[0, k]),
            pltpu.make_async_copy(acts.at[0, :, pl.ds(0, KSTEP)], a.at[k], load_sem.at[1, k]),
        ):
            load.wait()
        block = a[k]
        acc[...] += jnp.dot(block, w[k], preferred_element_type=F32)
        at[pl.ds(k * tiles, tiles)] = block.T.reshape(tiles, TILE, tokens)

    part = jnp.zeros((8, 128), F32)
    lane = lax.broadcasted_iota(jnp.int32, (128, 128), 1)
    names = lax.broadcasted_iota(jnp.int32, (128, classes), 1)
    for block in range(tokens // 128):
        rows = slice(block * 128, (block + 1) * 128)
        logits = acc[rows, :]
        hit = lab[rows, 0:1] == names
        top = jnp.max(logits, axis=1, keepdims=True)
        expo = jnp.exp(logits - top)
        total = jnp.sum(expo, axis=1, keepdims=True)
        lse = top + jnp.log(total)
        probs = expo * (1.0 / total)
        resid[rows, :] = jnp.where(hit, probs - 1.0, probs).astype(BF16)
        picked = jnp.where(hit, logits, 0.0)
        picked = sum(picked[:, 128 * i : 128 * (i + 1)] for i in range(classes // 128))
        each = jnp.where(lane == 0, lse, 0.0) - picked
        part = part + jnp.sum(each.reshape(16, 8, 128), axis=0)
    l1[core] = jnp.sum(part, axis=0, keepdims=True)

    pl.semaphore_wait(barrier, NC + NX + NZ - 3)

    def loss_copy(buf, mine, index, to, to_index):
        return pltpu.make_async_remote_copy(
            src_ref=buf.at[mine], dst_ref=buf.at[mine],
            send_sem=loss_send.at[index], recv_sem=loss_recv.at[to_index],
            device_id=to, device_id_type=MESH,
        )

    loss_stages = [
        [loss_copy(l1, core, 0, pair, 0)],
        [loss_copy(l2, x, i, along_x[i - 1], i) for i in range(1, NX)],
        [loss_copy(l3, z, NX + i - 1, along_z[i - 1], NX + i - 1) for i in range(1, NZ)],
    ]

    def loss_stage(step):
        if step > 0:
            for copy in loss_stages[step - 1]:
                copy.wait_recv()
            if step == 1:
                l2[x] = l1[0] + l1[1]
            elif step == 2:
                l3[z] = (l2[0] + l2[1]) + (l2[2] + l2[3])
            else:
                rows = [l3[i] for i in range(NZ)]
                while len(rows) > 1:
                    rows = [p + q for p, q in zip(rows[::2], rows[1::2])]
                whole = jnp.sum(rows[0], axis=1, keepdims=True) / F32(count_all)
                loss[...] = jnp.broadcast_to(whole, (1, 128))
        if step < 3:
            for copy in loss_stages[step]:
                copy.start()

    def terms(tile):
        lhs = jnp.concatenate([at[i * 9 + tile] for i in range(NX * NZ)], axis=0)
        out = jnp.dot(lhs, resid[...], preferred_element_type=F32)
        return out.reshape(NX * NZ, 2, ROWS, classes)

    def store(buf, chunk, value):
        buf[chunk] = value.reshape(NZ, NX, ROWS, classes)

    def pair_copy(i):
        return pltpu.make_async_remote_copy(
            src_ref=snd.at[i], dst_ref=r2.at[i],
            send_sem=pair_send.at[i], recv_sem=pair_recv.at[i],
            device_id=pair, device_id_type=MESH,
        )

    pair_copies = [pair_copy(i) for i in range(9)]

    def terms_for_pair(k):
        both = terms(k + 5 * mate)
        for half in range(2):
            store(snd, 2 * k + half, both[:, half])
            pair_copies[2 * k + half].start()

    def terms_for_own(k):
        both = terms(k + 5 * core)
        for half in range(2):
            store(own, 2 * k + half, both[:, half])

    def terms_for_both():
        both = terms(4)
        first = core == 0
        store(snd, 8, jnp.where(first, both[:, 1], both[:, 0]))
        pair_copies[8].start()
        store(own, 8, jnp.where(first, both[:, 0], both[:, 1]))

    sent = {}
    xs = {step: at_x(step) for step in (-1, 1, 2)}
    zs = {step: at_z(step) for step in (-3, -2, -1, 1, 2, 3, 4)}
    to_x = {1: along_x[0], -1: along_x[NX - 2]}
    to_z = {1: along_z[0], -1: along_z[NZ - 2]}
    SIDE = {1: 0, -1: 1}

    def send(i, name, d, src, dst, to):
        slot = SLOTS.index((name, d))
        copy = pltpu.make_async_remote_copy(
            src_ref=src, dst_ref=dst,
            send_sem=send_sem.at[i, slot], recv_sem=recv_sem.at[i, slot],
            device_id=to, device_id_type=MESH,
        )
        copy.start()
        sent[i, name, d] = copy

    def arrived(i, name, d):
        sent[i, name, d].wait_recv()

    def stage(i, step):
        wa = WIDTHS[i]
        ca, cb = pl.ds(0, wa), pl.ds(wa, classes - wa)
        far = 1 if i % 2 == 0 else -1
        halves_z = {1: pl.ds(0, NZ // 2), -1: pl.ds(NZ // 2, NZ // 2)}
        halves_x = {1: pl.ds(0, NX // 2), -1: pl.ds(NX // 2, NX // 2)}
        if step == 1:
            pair_copies[i].wait_recv()
            own[i] += r2[i]
            for d in (1, -1):
                send(i, "xa1", d, own.at[i, halves_z[d], xs[2], :, ca], xa1.at[i, SIDE[d], :, :, ca], to_x[d])
                send(i, "zb1", d, own.at[i, zs[4], halves_x[d], :, cb], zb1.at[i, SIDE[d], :, :, cb], to_z[d])
        elif step == 2:
            for d in (1, -1):
                arrived(i, "xa1", d)
                own[i, halves_z[d], xs[d], :, ca] += xa1[i, SIDE[d], :, :, ca]
            for d in (1, -1):
                send(i, "xa2", d, own.at[i, :, xs[d], :, ca], xa2.at[i, SIDE[d], :, :, ca], to_x[d])
            for d in (1, -1):
                arrived(i, "zb1", d)
                own[i, zs[3 * d], halves_x[d], :, cb] += zb1[i, SIDE[d], :, :, cb]
            for d in (1, -1):
                send(i, "zb2", d, own.at[i, zs[3 * d], :, :, cb], zb.at[i, 0, SIDE[d], :, :, cb], to_z[d])
        elif step == 3:
            for d in (1, -1):
                arrived(i, "xa2", d)
            own[i, :, x, :, ca] += xa2[i, 0, :, :, ca] + xa2[i, 1, :, :, ca]
            send(i, "za1", far, own.at[i, zs[4], x, :, ca], za1.at[i, :, ca], to_z[far])
            for d in (1, -1):
                arrived(i, "zb2", d)
                own[i, zs[2 * d], :, :, cb] += zb[i, 0, SIDE[d], :, :, cb]
                send(i, "zb3", d, own.at[i, zs[2 * d], :, :, cb], zb.at[i, 1, SIDE[d], :, :, cb], to_z[d])
        elif step == 4:
            arrived(i, "za1", far)
            own[i, zs[3 * far], x, :, ca] += za1[i, :, ca]
            for d in (1, -1):
                send(i, "za2", d, own.at[i, zs[3 * d], x, :, ca], za.at[i, 0, SIDE[d], :, ca], to_z[d])
            for d in (1, -1):
                arrived(i, "zb3", d)
                own[i, zs[d], :, :, cb] += zb[i, 1, SIDE[d], :, :, cb]
                send(i, "zb4", d, own.at[i, zs[d], :, :, cb], zb.at[i, 2, SIDE[d], :, :, cb], to_z[d])
        elif step == 5:
            for d in (1, -1):
                arrived(i, "za2", d)
                own[i, zs[2 * d], x, :, ca] += za[i, 0, SIDE[d], :, ca]
                send(i, "za3", d, own.at[i, zs[2 * d], x, :, ca], za.at[i, 1, SIDE[d], :, ca], to_z[d])
            for d in (1, -1):
                arrived(i, "zb4", d)
            own[i, z, :, :, cb] += zb[i, 2, 0, :, :, cb] + zb[i, 2, 1, :, :, cb]
            send(i, "xb1", far, own.at[i, z, xs[2], :, cb], xb1.at[i, :, cb], to_x[far])
        elif step == 6:
            for d in (1, -1):
                arrived(i, "za3", d)
                own[i, zs[d], x, :, ca] += za[i, 1, SIDE[d], :, ca]
                send(i, "za4", d, own.at[i, zs[d], x, :, ca], za.at[i, 2, SIDE[d], :, ca], to_z[d])
            arrived(i, "xb1", far)
            own[i, z, xs[far], :, cb] += xb1[i, :, cb]
            for d in (1, -1):
                send(i, "xb2", d, own.at[i, z, xs[d], :, cb], xb2.at[i, SIDE[d], :, cb], to_x[d])
        else:
            row = i * ROWS + core * ROWS if i < 8 else mate * (8 * ROWS)
            rows = pl.ds(pl.multiple_of(row, ROWS), ROWS)
            factor = F32(1.0 / count_all**0.5)
            for d in (1, -1):
                arrived(i, "za4", d)
            grads[rows, ca] = (own[i, z, x, :, ca] + (za[i, 2, 0, :, ca] + za[i, 2, 1, :, ca])) * factor
            for d in (1, -1):
                arrived(i, "xb2", d)
            grads[rows, cb] = (own[i, z, x, :, cb] + (xb2[i, 0, :, cb] + xb2[i, 1, :, cb])) * factor

    loss_stage(0)
    computes = [
        [lambda: terms_for_pair(0), lambda: terms_for_own(0), lambda: terms_for_pair(1)],
        [lambda: terms_for_own(1), lambda: terms_for_pair(2)],
        [lambda: terms_for_own(2), lambda: terms_for_pair(3)],
        [lambda: terms_for_own(3), terms_for_both],
    ]
    chunks = 9
    for slot in range(chunks + max(BEHIND.values())):
        if slot < len(computes):
            for compute in computes[slot]:
                compute()
        for step in range(1, 8):
            i = slot - BEHIND.get(step, 0)
            if 0 <= i < chunks:
                stage(i, step)
        if slot in (1, 3, 6):
            loss_stage({1: 1, 3: 2, 6: 3}[slot])

    for copy in pair_copies:
        copy.wait_send()
    for group in loss_stages:
        for copy in group:
            copy.wait_send()
    for copy in sent.values():
        copy.wait_send()


SLOTS = [
    (name, d)
    for name in ("xa1", "xa2", "za2", "za3", "za4", "zb1", "zb2", "zb3", "zb4", "xb2")
    for d in (1, -1)
]
SLOTS += [("za1", 1), ("za1", -1), ("xb1", 1), ("xb1", -1)]


def per_device(acts, probes, labels):
    tokens, depth = acts.shape[1:]
    classes = probes.shape[2]
    count_all = tokens * SHARDS
    n = depth // SHARDS // ROWS
    steps = depth // KSTEP
    vmem, sems = pltpu.VMEM, pltpu.SemaphoreType.DMA
    grads, loss = pl.pallas_call(
        lambda *refs: kernel(tokens, depth, classes, count_all, *refs),
        out_shape=(
            jax.ShapeDtypeStruct((depth // SHARDS, classes), F32),
            jax.ShapeDtypeStruct((1, 128), F32),
        ),
        in_specs=[
            pl.BlockSpec(memory_space=pl.ANY),
            pl.BlockSpec(memory_space=pl.ANY),
            pl.BlockSpec(memory_space=pltpu.VMEM),
        ],
        out_specs=(pl.BlockSpec(memory_space=pltpu.VMEM),) * 2,
        scratch_shapes=[
            vmem((steps, tokens, KSTEP), BF16),
            vmem((steps, KSTEP, classes), BF16),
            vmem((depth // TILE, TILE, tokens), BF16),
            vmem((tokens, classes), F32),
            vmem((tokens, classes), BF16),
            vmem((tokens, 128), jnp.int32),
            vmem((n, NZ, NX, ROWS, classes), F32),
            vmem((n, NZ, NX, ROWS, classes), F32),
            vmem((n, NZ, NX, ROWS, classes), F32),
            vmem((n, 2, NZ // 2, ROWS, classes), F32),
            vmem((n, 2, NZ, ROWS, classes), F32),
            vmem((n, ROWS, classes), F32),
            vmem((n, 3, 2, ROWS, classes), F32),
            vmem((n, 2, NX // 2, ROWS, classes), F32),
            vmem((n, 3, 2, NX, ROWS, classes), F32),
            vmem((n, ROWS, classes), F32),
            vmem((n, 2, ROWS, classes), F32),
            vmem((NC, 1, 128), F32),
            vmem((NX, 1, 128), F32),
            vmem((NZ, 1, 128), F32),
            sems((2, steps)),
            sems((n,)),
            sems((n,)),
            sems((n, len(SLOTS))),
            sems((n, len(SLOTS))),
            sems((NX + NZ - 1,)),
            sems((NX + NZ - 1,)),
        ],
        compiler_params=pltpu.CompilerParams(
            collective_id=0, has_side_effects=True, vmem_limit_bytes=62 * 1024 * 1024
        ),
        name="probe_step",
    )(acts, probes, labels.reshape(tokens // 128, 128))
    return grads[None], loss[0, :1]


def solution(mesh):
    return jax.shard_map(
        per_device,
        mesh=mesh,
        in_specs=(P("layer", "dp", None), P("layer", None, None), P("dp")),
        out_specs=(P("layer", "dp", None), P("layer")),
        check_vma=False,
    )
```

time: 198 us -> 71.9 us (0.36)
  the two profiles are of different devices: /device:TPU:27 before, /device:TPU:16 now
where the time goes in v1:
time: 71.9 us; the launch traced here: 71.7 us
  Pallas kernels  67.8 us (94%)
  between operations  2.39 us (3%)
  local copies, waits for them, and re-layouts  1.58 us (2%)
    pallas_call x1, Pallas kernels, per_device(): pl.pallas_call(lambda *refs: kernel(tokens, depth, classes, count_all, *r...  67.8 us
    unnamed x1, local copies, waits for them, and re-layouts  1.58 us

profile of v1, /device:TPU:16, one launch (start us, length us, event | category | flops | bytes accessed | tf_op | source)
XLA Modules:
  0.0 71.7 jit_solution(17609667646607592269)
XLA Ops:
  0.6 67.8 %probe_step.1 = (f32[72,512]{1,0:T(8,128)}, f32[1,128]{1,0:T(1,128)}) custom-call(bf16[1,896,4608]{2,1,0:T(8,128)(2,1)} %refs_0_.1, bf16[1,4608,512]{2,1,0:T(8,128)(2,1)} %refs_1_.1, s32[7,128]{1,0:T(8,128)} %bitcast.5), custom_call_target="tpu_custom_call" | custom-call | tf_op jit(solution)/shard_map/probe_step/pallas_call | solution.py:305
  68.4 1.6 %copy.7 = f32[1,72,512]{2,1,0:T(8,128)} copy(f32[1,72,512]{2,1,0:T(8,128)} %bitcast.4) | data formatting | bytes 294912

commit v2 on v1

v2 whole, which is shorter than its diff:
```python
import jax
import jax.numpy as jnp
from jax import lax
from jax.experimental import pallas as pl
from jax.experimental.pallas import tpu as pltpu
from jax.sharding import PartitionSpec as P

F32 = jnp.float32
BF16 = jnp.bfloat16
MESH = pl.DeviceIdType.MESH

NX, NZ, NC = 4, 8, 2
SHARDS = NX * NZ * NC
ROWS = 8
TILE = 16
KSTEP = 768
AHEAD = 2

WIDTHS = (256, 256, 384, 256, 256, 384, 256, 256, 384)
STEPS = {
    "x1": [[(2, 2), (1, 1)]],
    "x2": [[(2, 1)], [(1, 1)]],
    "z2": [[(4, 2), (3, 1)], [(2, 2), (1, 1)]],
    "z4": [[(4, 1)], [(3, 1)], [(2, 1)], [(1, 1)]],
}
PLANS = (
    ("x2", "z2", "z4", "x1"),
    ("x2", "z2", "z4", "x1"),
    ("x2", "z2", "z4", "x1"),
    ("x2", "z2", "z4", "x1"),
    ("x2", "z2", "z4", "x1"),
    ("x2", "z2", "z4", "x1"),
    ("x2", "z2", "z4", "x1"),
    ("x2", "z2", "z4", "x1"),
    ("x2", "z2", "z4", "x1"),
)
ORDER = (
    (0, 0, 0), (1, 0, 0), (0, 1, 0), (1, 1, 0), (5, 0, 0), (0, 2, 0), (3, 0, 0), (4, 0, 0),
    (1, 2, 0), (3, 1, 0), (4, 1, 0), (0, 3, 0), (1, 3, 0), (3, 2, 0), (4, 2, 0), (2, 0, 0),
    (5, 0, 1), (3, 3, 0), (4, 3, 0), (4, 0, 1), (3, 4, 0), (4, 4, 0), (3, 0, 1), (4, 1, 1),
    (3, 1, 1), (3, 5, 0), (4, 5, 0), (4, 2, 1), (3, 6, 0), (4, 6, 0), (3, 2, 1), (4, 3, 1),
    (3, 7, 0), (4, 7, 0), (3, 3, 1), (4, 0, 2), (3, 8, 0), (4, 4, 1), (3, 4, 1), (4, 8, 0),
    (4, 1, 2), (4, 5, 1), (4, 2, 2), (3, 0, 2), (4, 6, 1), (5, 0, 2), (4, 3, 2), (4, 7, 1),
    (3, 1, 2), (4, 0, 3), (3, 5, 1), (4, 4, 2), (4, 8, 1), (3, 6, 1), (4, 1, 3), (4, 5, 2),
    (4, 2, 3), (3, 0, 3), (3, 2, 2), (4, 6, 2), (3, 7, 1), (4, 3, 3), (4, 7, 2), (3, 1, 3),
    (3, 3, 2), (4, 0, 4), (5, 0, 3), (4, 4, 3), (3, 8, 1), (4, 8, 2), (4, 1, 4), (4, 5, 3),
    (3, 4, 2), (4, 2, 4), (3, 0, 4), (3, 2, 3), (3, 5, 2), (4, 6, 3), (4, 3, 4), (3, 6, 2),
    (4, 7, 3), (3, 1, 4), (3, 3, 3), (3, 7, 2), (4, 4, 4), (4, 8, 3), (4, 0, 5), (4, 5, 4),
    (3, 4, 3), (3, 2, 4), (3, 8, 2), (3, 5, 3), (4, 1, 5), (4, 6, 4), (4, 2, 5), (4, 3, 5),
    (3, 6, 3), (4, 4, 5), (4, 7, 4), (4, 5, 5), (3, 3, 4), (3, 7, 3), (4, 8, 4), (3, 4, 4),
    (3, 8, 3), (4, 6, 5), (3, 5, 4), (4, 7, 5), (3, 6, 4), (4, 8, 5), (3, 7, 4), (3, 8, 4),
)


def kernel(
    tokens, depth, classes, count_all,
    acts, probes, labels,
    grads, loss,
    a, w, at, acc, resid, lab, raw,
    snd, own, r2, xa2, xa1, za, zb4, zb, xb,
    l1, l2, l3, gauge, row_gauge,
    load_sem, label_sem, pair_send, pair_recv, send_sem, recv_sem, loss_send, loss_recv,
):
    dp = lax.axis_index("dp")
    core = lax.rem(dp, NC)
    chip = lax.div(dp, NC)
    x = lax.rem(chip, NX)
    z = lax.div(chip, NX)
    mate = 1 - core

    def at_x(step):
        return lax.rem(x + step + NX, NX)

    def at_z(step):
        return lax.rem(z + step + NZ, NZ)

    def device(zz, xx, cc):
        return {"dp": (zz * NX + xx) * NC + cc}

    pair = device(z, x, mate)
    along_x = [device(z, at_x(step), core) for step in range(1, NX)]
    along_z = [device(at_z(step), x, core) for step in range(1, NZ)]

    barrier = pltpu.get_barrier_semaphore()
    for peer in [pair] + along_x + along_z:
        pl.semaphore_signal(barrier, inc=1, device_id=peer, device_id_type=MESH)

    steps = depth // KSTEP
    tiles = KSTEP // TILE

    def loads(k):
        columns = pl.ds(pl.multiple_of(k * KSTEP, KSTEP), KSTEP)
        return (
            pltpu.make_async_copy(probes.at[0, columns, :], w.at[k], load_sem.at[0, k]),
            pltpu.make_async_copy(acts.at[0, :, columns], a.at[k], load_sem.at[1, k]),
        )

    for k in range(AHEAD):
        for load in loads(k):
            load.start()
    label_load = pltpu.make_async_copy(labels, raw, label_sem)
    label_load.start()

    acc[...] = jnp.zeros_like(acc)

    @pl.loop(0, steps)
    def _(k):
        for load in loads(k):
            load.wait()

        @pl.when(k + AHEAD < steps)
        def _():
            for load in loads(k + AHEAD):
                load.start()

        block = a[k]
        acc[...] += jnp.dot(block, w[k], preferred_element_type=F32)
        at[pl.ds(k * tiles, tiles)] = block.T.reshape(tiles, TILE, tokens)

    label_load.wait()
    for block in range(tokens // 128):
        row = jnp.broadcast_to(raw[block : block + 1, :], (128, 128))
        lab[block * 128 : (block + 1) * 128, :] = row.T
    part = jnp.zeros((8, 128), F32)
    lane = lax.broadcasted_iota(jnp.int32, (128, 128), 1)
    names = lax.broadcasted_iota(jnp.int32, (128, classes), 1)
    for block in range(tokens // 128):
        rows = slice(block * 128, (block + 1) * 128)
        logits = acc[rows, :]
        hit = lab[rows, 0:1] == names
        top = jnp.max(logits, axis=1, keepdims=True)
        expo = jnp.exp(logits - top)
        total = jnp.sum(expo, axis=1, keepdims=True)
        lse = top + jnp.log(total)
        probs = expo * (1.0 / total)
        resid[rows, :] = jnp.where(hit, probs - 1.0, probs).astype(BF16)
        picked = jnp.where(hit, logits, 0.0)
        picked = sum(picked[:, 128 * i : 128 * (i + 1)] for i in range(classes // 128))
        each = jnp.where(lane == 0, lse, 0.0) - picked
        part = part + jnp.sum(each.reshape(16, 8, 128), axis=0)
    l1[core] = jnp.sum(part, axis=0, keepdims=True)

    pl.semaphore_wait(barrier, NC + NX + NZ - 3)

    def whole_of(buf, count, sent_sem, got_sem):
        part = buf.at[pl.ds(0, count)]
        return pltpu.make_async_remote_copy(
            src_ref=part, dst_ref=part, send_sem=sent_sem, recv_sem=got_sem,
            device_id=pair, device_id_type=MESH,
        )

    def loss_copy(buf, mine, stage_index, to):
        return pltpu.make_async_remote_copy(
            src_ref=buf.at[mine], dst_ref=buf.at[mine],
            send_sem=loss_send, recv_sem=loss_recv.at[stage_index],
            device_id=to, device_id_type=MESH,
        )

    loss_stages = [
        [loss_copy(l1, core, 0, pair)],
        [loss_copy(l2, x, 1, to) for to in along_x],
        [loss_copy(l3, z, 2, to) for to in along_z],
    ]

    def loss_stage(step):
        if step > 0:
            whole_of(row_gauge, len(loss_stages[step - 1]), loss_send, loss_recv.at[step - 1]).wait_recv()
            if step == 1:
                l2[x] = l1[0] + l1[1]
            elif step == 2:
                l3[z] = (l2[0] + l2[1]) + (l2[2] + l2[3])
            else:
                rows = [l3[i] for i in range(NZ)]
                while len(rows) > 1:
                    rows = [p + q for p, q in zip(rows[::2], rows[1::2])]
                whole = jnp.sum(rows[0], axis=1, keepdims=True) / F32(count_all)
                loss[...] = jnp.broadcast_to(whole, (1, 128))
        if step < 3:
            for copy in loss_stages[step]:
                copy.start()

    def terms(tile):
        lhs = jnp.concatenate([at[i * 9 + tile] for i in range(NX * NZ)], axis=0)
        out = jnp.dot(lhs, resid[...], preferred_element_type=F32)
        return out.reshape(NX * NZ, 2, ROWS, classes)

    def store(buf, chunk, value):
        buf[chunk] = value.reshape(NZ, NX, ROWS, classes)

    def pair_copy(i):
        return pltpu.make_async_remote_copy(
            src_ref=snd.at[i], dst_ref=r2.at[i],
            send_sem=pair_send, recv_sem=pair_recv.at[i],
            device_id=pair, device_id_type=MESH,
        )

    pair_copies = [pair_copy(i) for i in range(9)]

    def terms_for_pair(k):
        both = terms(k + 5 * mate)
        for half in range(2):
            store(snd, 2 * k + half, both[:, half])
            pair_copies[2 * k + half].start()

    def terms_for_own(k):
        both = terms(k + 5 * core)
        for half in range(2):
            store(own, 2 * k + half, both[:, half])

    def terms_for_both():
        both = terms(4)
        first = core == 0
        store(snd, 8, jnp.where(first, both[:, 1], both[:, 0]))
        pair_copies[8].start()
        store(own, 8, jnp.where(first, both[:, 0], both[:, 1]))

    ring = {"x": (at_x, along_x, NX), "z": (at_z, along_z, NZ)}
    counts = []

    def size(i, stream, which, j):
        lanes = (WIDTHS[i] if stream == 0 else classes - WIDTHS[i]) // 128
        if which == 1:
            return lanes
        lanes *= NZ if stream == 0 else NX
        return lanes // 2 if j == (NX if stream == 0 else NZ) // 2 else lanes

    def slot(stream, step):
        return stream * MOST + step

    def parts(i, stream):
        wa = WIDTHS[i]
        plan = PLANS[i]
        if stream == 0:
            cols = pl.ds(0, wa)
            half = {1: pl.ds(0, NZ // 2), -1: pl.ds(NZ // 2, NZ // 2)}

            def first(j, d):
                if j == NX // 2:
                    side = (half[d], at_x(j * d), slice(None), cols)
                else:
                    side = (slice(None), at_x(j * d), slice(None), cols)
                return (i,) + side

            def first_land(j, d):
                if j == NX // 2:
                    return xa2, (i, SIDE[d], slice(None), slice(None), cols)
                return xa1, (i, SIDE[d], slice(None), slice(None), cols)

            def after(j, d, k):
                kept = half[d] if j == NX // 2 else slice(None)
                return (i, kept, at_x(k * d), slice(None), cols)

            def second(j, d):
                return (i, at_z(j * d), x, slice(None), cols)

            def second_land(j, d):
                return za, (i, j - 1, SIDE[d], slice(None), cols)

            return ("x", plan[0], first, first_land, after), ("z", plan[1], second, second_land, None)
        cols = pl.ds(wa, classes - wa)
        half = {1: pl.ds(0, NX // 2), -1: pl.ds(NX // 2, NX // 2)}

        def first(j, d):
            kept = half[d] if j == NZ // 2 else slice(None)
            return (i, at_z(j * d), kept, slice(None), cols)

        def first_land(j, d):
            if j == NZ // 2:
                return zb4, (i, SIDE[d], slice(None), slice(None), cols)
            return zb, (i, j - 1, SIDE[d], slice(None), slice(None), cols)

        def after(j, d, k):
            kept = half[d] if j == NZ // 2 else slice(None)
            return (i, at_z(k * d), kept, slice(None), cols)

        def second(j, d):
            return (i, z, at_x(j * d), slice(None), cols)

        def second_land(j, d):
            return xb, (i, j - 1, SIDE[d], slice(None), cols)

        return ("z", plan[2], first, first_land, after), ("x", plan[3], second, second_land, None)

    def moves(i, phase, big):
        far = 1 if i % 2 == 0 else -1
        axis, steps = phase[0], STEPS[phase[1]]
        top = ring[axis][2] // 2
        return [
            [(j, h, d) for j, h in step for d in (1, -1) if big or j < top or d == far]
            for step in steps
        ]

    def stage(i, stream, step):
        phases = parts(i, stream)
        todo = [(0, m) for m in moves(i, phases[0], True)] + [(1, m) for m in moves(i, phases[1], False)]
        if step == 0 and ready.setdefault(i, True):
            pair_copies[i].wait_recv()
            own[i] += r2[i]
            ready[i] = False
        if step > 0:
            which, group = todo[step - 1]
            axis, _, place, land, after = phases[which]
            finals = []
            count = sum(size(i, stream, which, j) for j, h, d in group)
            whole_of(gauge, count, send_sem, recv_sem.at[i, slot(stream, step - 1)]).wait_recv()
            for j, h, d in group:
                buf, index = land(j, d)
                if j == h:
                    finals.append((buf, index, j, d))
                else:
                    spot = after(j, d, j - h) if after else place(j - h, d)
                    own[spot] += buf[index]
            last.setdefault((i, stream, which), []).extend(finals)
            if step == len(todo) or todo[step][0] != which:
                finals = last[i, stream, which]
                top = ring[axis][2] // 2
                if which == 0:
                    whole = [buf[index] for buf, index, j, d in finals if j < top]
                    spot = place(0, 1)
                    total = own[spot]
                    for value in whole:
                        total += value
                    own[spot] = total
                    for buf, index, j, d in finals:
                        if j == top:
                            own[after(j, d, 0)] += buf[index]
                else:
                    total = own[place(0, 1)]
                    for buf, index, j, d in finals:
                        total += buf[index]
                    row = i * ROWS + core * ROWS if i < 8 else mate * (8 * ROWS)
                    rows = pl.ds(pl.multiple_of(row, ROWS), ROWS)
                    grads[rows, index[-1]] = total * F32(1.0 / count_all**0.5)
        if step < len(todo):
            which, group = todo[step]
            axis, _, place, land, _ = phases[which]
            _, peers, _ = ring[axis]
            for j, h, d in group:
                buf, index = land(j, d)
                copy = pltpu.make_async_remote_copy(
                    src_ref=own.at[place(j, d)], dst_ref=buf.at[index],
                    send_sem=send_sem, recv_sem=recv_sem.at[i, slot(stream, step)],
                    device_id=peers[h - 1 if d > 0 else len(peers) - h], device_id_type=MESH,
                )
                copy.start()
                counts.append(size(i, stream, which, j))

    SIDE = {1: 0, -1: 1}
    ready, last = {}, {}
    for code, i, step in ORDER:
        if code == 0:
            terms_for_pair(i)
        elif code == 1:
            terms_for_own(i)
        elif code == 2:
            terms_for_both()
        elif code == 5:
            loss_stage(step)
        else:
            stage(i, code - 3, step)

    pltpu.make_async_remote_copy(
        src_ref=snd, dst_ref=r2, send_sem=pair_send, recv_sem=pair_recv.at[0],
        device_id=pair, device_id_type=MESH,
    ).wait_send()
    whole_of(row_gauge, sum(len(group) for group in loss_stages), loss_send, loss_recv.at[0]).wait_send()
    assert sum(counts) == copied_tiles(classes)
    whole_of(gauge, sum(counts), send_sem, recv_sem.at[0, 0]).wait_send()


def copied_tiles(classes):
    total = 0
    for width, plan in zip(WIDTHS, PLANS):
        for lanes, first, second, n, m in (
            (width // 128, plan[0], plan[1], NX, NZ),
            ((classes - width) // 128, plan[2], plan[3], NZ, NX),
        ):
            for steps in STEPS[first]:
                total += sum(lanes * m * (1 if j == n // 2 else 2) for j, h in steps)
            for steps in STEPS[second]:
                total += sum(lanes * (1 if j == m // 2 else 2) for j, h in steps)
    return total


MOST = 5


def per_device(acts, probes, labels):
    tokens, depth = acts.shape[1:]
    classes = probes.shape[2]
    count_all = tokens * SHARDS
    n = depth // SHARDS // ROWS
    steps = depth // KSTEP
    vmem, sems = pltpu.VMEM, pltpu.SemaphoreType.DMA
    grads, loss = pl.pallas_call(
        lambda *refs: kernel(tokens, depth, classes, count_all, *refs),
        out_shape=(
            jax.ShapeDtypeStruct((depth // SHARDS, classes), F32),
            jax.ShapeDtypeStruct((1, 128), F32),
        ),
        in_specs=[
            pl.BlockSpec(memory_space=pl.ANY),
            pl.BlockSpec(memory_space=pl.ANY),
            pl.BlockSpec(memory_space=pl.ANY),
        ],
        out_specs=(pl.BlockSpec(memory_space=pltpu.VMEM),) * 2,
        scratch_shapes=[
            vmem((steps, tokens, KSTEP), BF16),
            vmem((steps, KSTEP, classes), BF16),
            vmem((depth // TILE, TILE, tokens), BF16),
            vmem((tokens, classes), F32),
            vmem((tokens, classes), BF16),
            vmem((tokens, 128), jnp.int32),
            vmem((tokens // 128, 128), jnp.int32),
            vmem((n, NZ, NX, ROWS, classes), F32),
            vmem((n, NZ, NX, ROWS, classes), F32),
            vmem((n, NZ, NX, ROWS, classes), F32),
            vmem((n, 2, NZ // 2, ROWS, classes), F32),
            vmem((n, 2, NZ, ROWS, classes), F32),
            vmem((n, 4, 2, ROWS, classes), F32),
            vmem((n, 2, NX // 2, ROWS, classes), F32),
            vmem((n, 3, 2, NX, ROWS, classes), F32),
            vmem((n, 2, 2, ROWS, classes), F32),
            vmem((NC, 1, 128), F32),
            vmem((NX, 1, 128), F32),
            vmem((NZ, 1, 128), F32),
            vmem((copied_tiles(classes), 8, 128), F32),
            vmem((16, 1, 128), F32),
            sems((2, steps)),
            sems(()),
            sems(()),
            sems((n,)),
            sems(()),
            sems((n, 2 * MOST)),
            sems(()),
            sems((3,)),
        ],
        compiler_params=pltpu.CompilerParams(
            collective_id=0, has_side_effects=True, vmem_limit_bytes=62 * 1024 * 1024
        ),
        name="probe_step",
    )(acts, probes, labels.reshape(tokens // 128, 128))
    return grads[None], loss[0, :1]


def solution(mesh):
    return jax.shard_map(
        per_device,
        mesh=mesh,
        in_specs=(P("layer", "dp", None), P("layer", None, None), P("dp")),
        out_specs=(P("layer", "dp", None), P("layer")),
        check_vma=False,
    )
```

time: 71.9 us -> 56.9 us (0.79)
  Pallas kernels: 67.8 us -> 52.8 us
    pallas_call x1, Pallas kernels: 67.8 us -> 52.8 us  [per_device(): pl.pallas_call(lambda *refs: kernel(tokens, depth, classes, count_all, *r...]
where the time goes in v2:
time: 56.9 us; the launch traced here: 56.8 us
  Pallas kernels  52.8 us (93%)
  between operations  2.39 us (4%)
  local copies, waits for them, and re-layouts  1.58 us (3%)
    pallas_call x1, Pallas kernels, per_device(): pl.pallas_call(lambda *refs: kernel(tokens, depth, classes, count_all, *r...  52.8 us
    unnamed x1, local copies, waits for them, and re-layouts  1.58 us

profile of v2, /device:TPU:16, one launch (start us, length us, event | category | flops | bytes accessed | tf_op | source)
XLA Modules:
  0.0 56.8 jit_solution(11381512216572674106)
XLA Ops:
  0.6 52.8 %probe_step.1 = (f32[72,512]{1,0:T(8,128)}, f32[1,128]{1,0:T(1,128)}) custom-call(bf16[1,896,4608]{2,1,0:T(8,128)(2,1)} %refs_0_.1, bf16[1,4608,512]{2,1,0:T(8,128)(2,1)} %refs_1_.1, s32[7,128]{1,0:T(8,128)} %bitcast.5), custom_call_target="tpu_custom_call" | custom-call | tf_op jit(solution)/shard_map/probe_step/pallas_call | solution.py:395
  53.4 1.6 %copy.7 = f32[1,72,512]{2,1,0:T(8,128)} copy(f32[1,72,512]{2,1,0:T(8,128)} %bitcast.4) | data formatting | bytes 294912

commit v3 on v2

--- a/solution.py
+++ b/solution.py
@@ -16,39 +16,42 @@
 KSTEP = 768
 AHEAD = 2
 
-WIDTHS = (256, 256, 384, 256, 256, 384, 256, 256, 384)
+WIDTHS = (128, 256, 256, 384, 384, 384, 128, 384, 256)
 STEPS = {
     "x1": [[(2, 2), (1, 1)]],
     "x2": [[(2, 1)], [(1, 1)]],
+    "z1": [[(4, 4), (3, 3), (2, 2), (1, 1)]],
     "z2": [[(4, 2), (3, 1)], [(2, 2), (1, 1)]],
+    "z3": [[(4, 2), (3, 1)], [(2, 1)], [(1, 1)]],
     "z4": [[(4, 1)], [(3, 1)], [(2, 1)], [(1, 1)]],
 }
 PLANS = (
+    ("x1", "z3", "z4", "x1"),
+    ("x2", "z4", "z3", "x2"),
+    ("x2", "z4", "z3", "x2"),
+    ("x2", "z4", "z4", "x2"),
+    ("x2", "z3", "z4", "x1"),
+    ("x2", "z3", "z2", "x2"),
     ("x2", "z2", "z4", "x1"),
-    ("x2", "z2", "z4", "x1"),
-    ("x2", "z2", "z4", "x1"),
-    ("x2", "z2", "z4", "x1"),
-    ("x2", "z2", "z4", "x1"),
-    ("x2", "z2", "z4", "x1"),
-    ("x2", "z2", "z4", "x1"),
-    ("x2", "z2", "z4", "x1"),
-    ("x2", "z2", "z4", "x1"),
+    ("x2", "z2", "z4", "x2"),
+    ("x2", "z1", "z4", "x1"),
 )
 ORDER = (
     (0, 0, 0), (1, 0, 0), (0, 1, 0), (1, 1, 0), (5, 0, 0), (0, 2, 0), (3, 0, 0), (4, 0, 0),
     (1, 2, 0), (3, 1, 0), (4, 1, 0), (0, 3, 0), (1, 3, 0), (3, 2, 0), (4, 2, 0), (2, 0, 0),
-    (5, 0, 1), (3, 3, 0), (4, 3, 0), (4, 0, 1), (3, 4, 0), (4, 4, 0), (3, 0, 1), (4, 1, 1),
-    (3, 1, 1), (3, 5, 0), (4, 5, 0), (4, 2, 1), (3, 6, 0), (4, 6, 0), (3, 2, 1), (4, 3, 1),
-    (3, 7, 0), (4, 7, 0), (3, 3, 1), (4, 0, 2), (3, 8, 0), (4, 4, 1), (3, 4, 1), (4, 8, 0),
-    (4, 1, 2), (4, 5, 1), (4, 2, 2), (3, 0, 2), (4, 6, 1), (5, 0, 2), (4, 3, 2), (4, 7, 1),
-    (3, 1, 2), (4, 0, 3), (3, 5, 1), (4, 4, 2), (4, 8, 1), (3, 6, 1), (4, 1, 3), (4, 5, 2),
-    (4, 2, 3), (3, 0, 3), (3, 2, 2), (4, 6, 2), (3, 7, 1), (4, 3, 3), (4, 7, 2), (3, 1, 3),
-    (3, 3, 2), (4, 0, 4), (5, 0, 3), (4, 4, 3), (3, 8, 1), (4, 8, 2), (4, 1, 4), (4, 5, 3),
-    (3, 4, 2), (4, 2, 4), (3, 0, 4), (3, 2, 3), (3, 5, 2), (4, 6, 3), (4, 3, 4), (3, 6, 2),
-    (4, 7, 3), (3, 1, 4), (3, 3, 3), (3, 7, 2), (4, 4, 4), (4, 8, 3), (4, 0, 5), (4, 5, 4),
-    (3, 4, 3), (3, 2, 4), (3, 8, 2), (3, 5, 3), (4, 1, 5), (4, 6, 4), (4, 2, 5), (4, 3, 5),
-    (3, 6, 3), (4, 4, 5), (4, 7, 4), (4, 5, 5), (3, 3, 4), (3, 7, 3), (4, 8, 4), (3, 4, 4),
-    (3, 8, 3), (4, 6, 5), (3, 5, 4), (4, 7, 5), (3, 6, 4), (4, 8, 5), (3, 7, 4), (3, 8, 4),
+    (5, 0, 1), (3, 3, 0), (4, 3, 0), (3, 4, 0), (4, 4, 0), (4, 0, 1), (3, 5, 0), (4, 5, 0),
+    (3, 0, 1), (3, 1, 1), (4, 1, 1), (3, 6, 0), (4, 6, 0), (3, 2, 1), (3, 7, 0), (4, 7, 0),
+    (4, 2, 1), (4, 3, 1), (3, 3, 1), (4, 4, 1), (3, 8, 0), (4, 8, 0), (3, 4, 1), (4, 0, 2),
+    (5, 0, 2), (4, 5, 1), (3, 5, 1), (3, 0, 2), (4, 1, 2), (4, 6, 1), (4, 7, 1), (3, 1, 2),
+    (3, 6, 1), (4, 2, 2), (4, 3, 2), (4, 4, 2), (4, 8, 1), (3, 2, 2), (4, 0, 3), (3, 7, 1),
+    (4, 5, 2), (3, 0, 3), (4, 1, 3), (3, 3, 2), (5, 0, 3), (3, 8, 1), (4, 6, 2), (4, 7, 2),
+    (3, 1, 3), (4, 2, 3), (4, 3, 3), (4, 4, 3), (3, 4, 2), (4, 8, 2), (3, 2, 3), (4, 0, 4),
+    (3, 0, 4), (3, 3, 3), (3, 5, 2), (3, 6, 2), (4, 6, 3), (4, 7, 3), (3, 1, 4), (4, 3, 4),
+    (4, 4, 4), (3, 4, 3), (3, 7, 2), (4, 5, 3), (4, 1, 4), (4, 8, 3), (3, 2, 4), (3, 3, 4),
+    (3, 5, 3), (4, 2, 4), (3, 8, 2), (3, 6, 3), (4, 3, 5), (4, 0, 5), (4, 6, 4), (4, 7, 4),
+    (4, 5, 4), (3, 1, 5), (4, 4, 5), (4, 1, 5), (3, 4, 4), (3, 7, 3), (4, 2, 5), (4, 8, 4),
+    (3, 2, 5), (4, 3, 6), (3, 3, 5), (3, 5, 4), (4, 7, 5), (4, 6, 5), (3, 8, 3), (3, 1, 6),
+    (3, 4, 5), (3, 6, 4), (3, 7, 4), (3, 2, 6), (4, 8, 5), (3, 3, 6), (4, 7, 6), (3, 5, 5),
 )
 
 
@@ -127,7 +130,7 @@
     for block in range(tokens // 128):
         rows = slice(block * 128, (block + 1) * 128)
         logits = acc[rows, :]
-        hit = lab[rows, 0:1] == names
+        hit = jnp.concatenate([lab[rows, :]] * (classes // 128), axis=1) == names
         top = jnp.max(logits, axis=1, keepdims=True)
         expo = jnp.exp(logits - top)
         total = jnp.sum(expo, axis=1, keepdims=True)
@@ -382,7 +385,7 @@
     return total
 
 
-MOST = 5
+MOST = 6
 
 
 def per_device(acts, probes, labels):

time: 56.9 us -> 55.3 us (0.972)
  Pallas kernels: 52.8 us -> 51.2 us
    pallas_call x1, Pallas kernels: 52.8 us -> 51.2 us  [per_device(): pl.pallas_call(lambda *refs: kernel(tokens, depth, classes, count_all, *r...]
where the time goes in v3:
time: 55.3 us; the launch traced here: 55.2 us
  Pallas kernels  51.2 us (93%)
  between operations  2.39 us (4%)
  local copies, waits for them, and re-layouts  1.58 us (3%)
    pallas_call x1, Pallas kernels, per_device(): pl.pallas_call(lambda *refs: kernel(tokens, depth, classes, count_all, *r...  51.2 us
    unnamed x1, local copies, waits for them, and re-layouts  1.58 us

profile of v3, /device:TPU:16, one launch (start us, length us, event | category | flops | bytes accessed | tf_op | source)
XLA Modules:
  0.0 55.2 jit_solution(13269369408484851324)
XLA Ops:
  0.6 51.2 %probe_step.1 = (f32[72,512]{1,0:T(8,128)}, f32[1,128]{1,0:T(1,128)}) custom-call(bf16[1,896,4608]{2,1,0:T(8,128)(2,1)} %refs_0_.1, bf16[1,4608,512]{2,1,0:T(8,128)(2,1)} %refs_1_.1, s32[7,128]{1,0:T(8,128)} %bitcast.5), custom_call_target="tpu_custom_call" | custom-call | tf_op jit(solution)/shard_map/probe_step/pallas_call | solution.py:398
  51.8 1.6 %copy.7 = f32[1,72,512]{2,1,0:T(8,128)} copy(f32[1,72,512]{2,1,0:T(8,128)} %bitcast.4) | data formatting | bytes 294912

commit v4 on v3

--- a/solution.py
+++ b/solution.py
@@ -16,42 +16,35 @@
 KSTEP = 768
 AHEAD = 2
 
-WIDTHS = (128, 256, 256, 384, 384, 384, 128, 384, 256)
+GROUPS = ((0, 1), (1, 1), (2, 2), (4, 2), (6, 2), (8, 1))
+WIDTHS = (384, 128, 256, 384, 256, 384)
 STEPS = {
     "x1": [[(2, 2), (1, 1)]],
     "x2": [[(2, 1)], [(1, 1)]],
-    "z1": [[(4, 4), (3, 3), (2, 2), (1, 1)]],
     "z2": [[(4, 2), (3, 1)], [(2, 2), (1, 1)]],
     "z3": [[(4, 2), (3, 1)], [(2, 1)], [(1, 1)]],
     "z4": [[(4, 1)], [(3, 1)], [(2, 1)], [(1, 1)]],
 }
 PLANS = (
-    ("x1", "z3", "z4", "x1"),
-    ("x2", "z4", "z3", "x2"),
-    ("x2", "z4", "z3", "x2"),
-    ("x2", "z4", "z4", "x2"),
-    ("x2", "z3", "z4", "x1"),
-    ("x2", "z3", "z2", "x2"),
+    ("x2", "z4", "z3", "x1"),
+    ("x1", "z3", "z3", "x2"),
+    ("x2", "z4", "z4", "x1"),
+    ("x2", "z3", "z3", "x2"),
     ("x2", "z2", "z4", "x1"),
-    ("x2", "z2", "z4", "x2"),
-    ("x2", "z1", "z4", "x1"),
+    ("x2", "z2", "z4", "x1"),
 )
 ORDER = (
     (0, 0, 0), (1, 0, 0), (0, 1, 0), (1, 1, 0), (5, 0, 0), (0, 2, 0), (3, 0, 0), (4, 0, 0),
-    (1, 2, 0), (3, 1, 0), (4, 1, 0), (0, 3, 0), (1, 3, 0), (3, 2, 0), (4, 2, 0), (2, 0, 0),
-    (5, 0, 1), (3, 3, 0), (4, 3, 0), (3, 4, 0), (4, 4, 0), (4, 0, 1), (3, 5, 0), (4, 5, 0),
-    (3, 0, 1), (3, 1, 1), (4, 1, 1), (3, 6, 0), (4, 6, 0), (3, 2, 1), (3, 7, 0), (4, 7, 0),
-    (4, 2, 1), (4, 3, 1), (3, 3, 1), (4, 4, 1), (3, 8, 0), (4, 8, 0), (3, 4, 1), (4, 0, 2),
-    (5, 0, 2), (4, 5, 1), (3, 5, 1), (3, 0, 2), (4, 1, 2), (4, 6, 1), (4, 7, 1), (3, 1, 2),
-    (3, 6, 1), (4, 2, 2), (4, 3, 2), (4, 4, 2), (4, 8, 1), (3, 2, 2), (4, 0, 3), (3, 7, 1),
-    (4, 5, 2), (3, 0, 3), (4, 1, 3), (3, 3, 2), (5, 0, 3), (3, 8, 1), (4, 6, 2), (4, 7, 2),
-    (3, 1, 3), (4, 2, 3), (4, 3, 3), (4, 4, 3), (3, 4, 2), (4, 8, 2), (3, 2, 3), (4, 0, 4),
-    (3, 0, 4), (3, 3, 3), (3, 5, 2), (3, 6, 2), (4, 6, 3), (4, 7, 3), (3, 1, 4), (4, 3, 4),
-    (4, 4, 4), (3, 4, 3), (3, 7, 2), (4, 5, 3), (4, 1, 4), (4, 8, 3), (3, 2, 4), (3, 3, 4),
-    (3, 5, 3), (4, 2, 4), (3, 8, 2), (3, 6, 3), (4, 3, 5), (4, 0, 5), (4, 6, 4), (4, 7, 4),
-    (4, 5, 4), (3, 1, 5), (4, 4, 5), (4, 1, 5), (3, 4, 4), (3, 7, 3), (4, 2, 5), (4, 8, 4),
-    (3, 2, 5), (4, 3, 6), (3, 3, 5), (3, 5, 4), (4, 7, 5), (4, 6, 5), (3, 8, 3), (3, 1, 6),
-    (3, 4, 5), (3, 6, 4), (3, 7, 4), (3, 2, 6), (4, 8, 5), (3, 3, 6), (4, 7, 6), (3, 5, 5),
+    (1, 2, 0), (3, 1, 0), (4, 1, 0), (0, 3, 0), (1, 3, 0), (2, 0, 0), (3, 2, 0), (5, 0, 1),
+    (4, 2, 0), (4, 0, 1), (3, 0, 1), (3, 3, 0), (4, 3, 0), (3, 1, 1), (4, 1, 1), (3, 4, 0),
+    (4, 4, 0), (4, 2, 1), (3, 2, 1), (3, 5, 0), (4, 5, 0), (4, 0, 2), (4, 3, 1), (5, 0, 2),
+    (3, 0, 2), (3, 1, 2), (4, 1, 2), (4, 4, 1), (3, 3, 1), (4, 2, 2), (3, 4, 1), (4, 5, 1),
+    (4, 0, 3), (4, 3, 2), (3, 0, 3), (3, 1, 3), (4, 1, 3), (3, 2, 2), (5, 0, 3), (3, 5, 1),
+    (4, 4, 2), (4, 2, 3), (4, 5, 2), (4, 3, 3), (3, 0, 4), (3, 1, 4), (3, 2, 3), (3, 3, 2),
+    (4, 4, 3), (4, 2, 4), (3, 4, 2), (4, 5, 3), (3, 0, 5), (4, 1, 4), (3, 2, 4), (4, 0, 4),
+    (3, 3, 3), (3, 5, 2), (4, 3, 4), (4, 4, 4), (4, 2, 5), (3, 4, 3), (4, 1, 5), (4, 5, 4),
+    (3, 0, 6), (3, 2, 5), (3, 3, 4), (4, 3, 5), (3, 5, 3), (4, 4, 5), (3, 4, 4), (4, 5, 5),
+    (3, 2, 6), (3, 3, 5), (3, 5, 4),
 )
 
 
@@ -221,7 +214,7 @@
     counts = []
 
     def size(i, stream, which, j):
-        lanes = (WIDTHS[i] if stream == 0 else classes - WIDTHS[i]) // 128
+        lanes = (WIDTHS[i] if stream == 0 else classes - WIDTHS[i]) // 128 * GROUPS[i][1]
         if which == 1:
             return lanes
         lanes *= NZ if stream == 0 else NX
@@ -231,6 +224,7 @@
         return stream * MOST + step
 
     def parts(i, stream):
+        span = pl.ds(*GROUPS[i])
         wa = WIDTHS[i]
         plan = PLANS[i]
         if stream == 0:
@@ -242,22 +236,22 @@
                     side = (half[d], at_x(j * d), slice(None), cols)
                 else:
                     side = (slice(None), at_x(j * d), slice(None), cols)
-                return (i,) + side
+                return (span,) + side
 
             def first_land(j, d):
                 if j == NX // 2:
-                    return xa2, (i, SIDE[d], slice(None), slice(None), cols)
-                return xa1, (i, SIDE[d], slice(None), slice(None), cols)
+                    return xa2, (span, SIDE[d], slice(None), slice(None), cols)
+                return xa1, (span, SIDE[d], slice(None), slice(None), cols)
 
             def after(j, d, k):
                 kept = half[d] if j == NX // 2 else slice(None)
-                return (i, kept, at_x(k * d), slice(None), cols)
+                return (span, kept, at_x(k * d), slice(None), cols)
 
             def second(j, d):
-                return (i, at_z(j * d), x, slice(None), cols)
+                return (span, at_z(j * d), x, slice(None), cols)
 
             def second_land(j, d):
-                return za, (i, j - 1, SIDE[d], slice(None), cols)
+                return za, (span, j - 1, SIDE[d], slice(None), cols)
 
             return ("x", plan[0], first, first_land, after), ("z", plan[1], second, second_land, None)
         cols = pl.ds(wa, classes - wa)
@@ -265,22 +259,22 @@
 
         def first(j, d):
             kept = half[d] if j == NZ // 2 else slice(None)
-            return (i, at_z(j * d), kept, slice(None), cols)
+            return (span, at_z(j * d), kept, slice(None), cols)
 
         def first_land(j, d):
             if j == NZ // 2:
-                return zb4, (i, SIDE[d], slice(None), slice(None), cols)
-            return zb, (i, j - 1, SIDE[d], slice(None), slice(None), cols)
+                return zb4, (span, SIDE[d], slice(None), slice(None), cols)
+            return zb, (span, j - 1, SIDE[d], slice(None), slice(None), cols)
 
         def after(j, d, k):
             kept = half[d] if j == NZ // 2 else slice(None)
-            return (i, at_z(k * d), kept, slice(None), cols)
+            return (span, at_z(k * d), kept, slice(None), cols)
 
         def second(j, d):
-            return (i, z, at_x(j * d), slice(None), cols)
+            return (span, z, at_x(j * d), slice(None), cols)
 
         def second_land(j, d):
-            return xb, (i, j - 1, SIDE[d], slice(None), cols)
+            return xb, (span, j - 1, SIDE[d], slice(None), cols)
 
         return ("z", plan[2], first, first_land, after), ("x", plan[3], second, second_land, None)
 
@@ -297,8 +291,9 @@
         phases = parts(i, stream)
         todo = [(0, m) for m in moves(i, phases[0], True)] + [(1, m) for m in moves(i, phases[1], False)]
         if step == 0 and ready.setdefault(i, True):
-            pair_copies[i].wait_recv()
-            own[i] += r2[i]
+            for chunk in range(GROUPS[i][0], sum(GROUPS[i])):
+                pair_copies[chunk].wait_recv()
+                own[chunk] += r2[chunk]
             ready[i] = False
         if step > 0:
             which, group = todo[step - 1]
@@ -331,8 +326,10 @@
                     total = own[place(0, 1)]
                     for buf, index, j, d in finals:
                         total += buf[index]
-                    row = i * ROWS + core * ROWS if i < 8 else mate * (8 * ROWS)
-                    rows = pl.ds(pl.multiple_of(row, ROWS), ROWS)
+                    chunk, height = GROUPS[i][0], GROUPS[i][1] * ROWS
+                    row = (chunk + core) * ROWS if chunk < 8 else mate * (8 * ROWS)
+                    rows = pl.ds(pl.multiple_of(row, ROWS), height)
+                    total = total.reshape(height, total.shape[-1])
                     grads[rows, index[-1]] = total * F32(1.0 / count_all**0.5)
         if step < len(todo):
             which, group = todo[step]
@@ -373,10 +370,10 @@
 
 def copied_tiles(classes):
     total = 0
-    for width, plan in zip(WIDTHS, PLANS):
+    for (_, height), width, plan in zip(GROUPS, WIDTHS, PLANS):
         for lanes, first, second, n, m in (
-            (width // 128, plan[0], plan[1], NX, NZ),
-            ((classes - width) // 128, plan[2], plan[3], NZ, NX),
+            (width // 128 * height, plan[0], plan[1], NX, NZ),
+            ((classes - width) // 128 * height, plan[2], plan[3], NZ, NX),
         ):
             for steps in STEPS[first]:
                 total += sum(lanes * m * (1 if j == n // 2 else 2) for j, h in steps)
@@ -434,7 +431,7 @@
             sems(()),
             sems((n,)),
             sems(()),
-            sems((n, 2 * MOST)),
+            sems((len(GROUPS), 2 * MOST)),
             sems(()),
             sems((3,)),
         ],

time: 55.3 us -> 55.9 us (1.011)
  Pallas kernels: 51.2 us -> 51.8 us
    pallas_call x1, Pallas kernels: 51.2 us -> 51.8 us  [per_device(): pl.pallas_call(lambda *refs: kernel(tokens, depth, classes, count_all, *r...]
where the time goes in v4:
time: 55.9 us; the launch traced here: 55.8 us
  Pallas kernels  51.8 us (93%)
  between operations  2.39 us (4%)
  local copies, waits for them, and re-layouts  1.58 us (3%)
    pallas_call x1, Pallas kernels, per_device(): pl.pallas_call(lambda *refs: kernel(tokens, depth, classes, count_all, *r...  51.8 us
    unnamed x1, local copies, waits for them, and re-layouts  1.58 us

profile of v4, /device:TPU:16, one launch (start us, length us, event | category | flops | bytes accessed | tf_op | source)
XLA Modules:
  0.0 55.8 jit_solution(11160022997432612220)
XLA Ops:
  0.6 51.8 %probe_step.1 = (f32[72,512]{1,0:T(8,128)}, f32[1,128]{1,0:T(1,128)}) custom-call(bf16[1,896,4608]{2,1,0:T(8,128)(2,1)} %refs_0_.1, bf16[1,4608,512]{2,1,0:T(8,128)(2,1)} %refs_1_.1, s32[7,128]{1,0:T(8,128)} %bitcast.5), custom_call_target="tpu_custom_call" | custom-call | tf_op jit(solution)/shard_map/probe_step/pallas_call | solution.py:395
  52.5 1.6 %copy.7 = f32[1,72,512]{2,1,0:T(8,128)} copy(f32[1,72,512]{2,1,0:T(8,128)} %bitcast.4) | data formatting | bytes 294912
